TPU v7x, 32 devices: a whole 2x2x4 slice. The times are simulated.
32 devices in a mesh: row: 4 (over x, core), col: 8 (over z, y).
Axes of the slice: x: 2, y: 2, z: 4, core: 2. Of those that a mesh axis runs over, the one named last changes fastest.
Arguments:
- tensor: float32 [1024, 32, 1024], P(None, 'row', 'col'), may hold values from -60 to 60, as said below
- factor_two: float32 [32, 32], P('row'), may hold values from -1 to 1
- factor_three: float32 [32, 32], P('col'), may hold values from -1 to 1
- factor_four: float32 [32, 16], replicated, may hold values from -1 to 1
- factor_init: float32 [1024, 64], replicated, may hold values from -6 to 6
Outputs:
- factor_new: float32 [1024, 64], replicated
- core: float32 [64, 32, 32, 16], P(None, 'row', 'col')
Inputs may be any that keep to these rules, and one draw needn't show every extreme that they name: `tensor`: scales vary from slab to slab.
All inputs are finite; a program needn't handle non-finite values.
Results may differ from a plain program's by a relative error of at most 0.00013.
Values sent between devices are 32-bit elements; how exact they have to be, the bound alone decides.
A program may use at most 128 MiB of HBM per device.

v0:
```python
import jax
import jax.numpy as jnp
from jax import lax
from jax.sharding import PartitionSpec as P


def shards(tensor, factor_two, factor_three, factor_four, factor_init):
    highest = lax.Precision.HIGHEST
    first_len = tensor.shape[0]
    local_two = tensor.shape[1]
    fourth_len = factor_four.shape[0]
    local_three = tensor.shape[2] // fourth_len
    rank_one = factor_init.shape[1]
    data = tensor.reshape(first_len, local_two, local_three, fourth_len)
    fourth = jnp.einsum("abcd,de->abce", data, factor_four, precision=highest)
    whole_two = lax.all_gather(factor_two, "row", axis=0, tiled=True)
    spread_two = lax.all_to_all(fourth, "row", split_axis=0, concat_axis=1, tiled=True)
    projected_two = jnp.einsum("abce,bg->agce", spread_two, whole_two, precision=highest)
    partial_two = lax.all_to_all(projected_two, "row", split_axis=1, concat_axis=0, tiled=True)
    whole_three = lax.all_gather(factor_three, "col", axis=0, tiled=True)
    spread_three = lax.all_to_all(partial_two, "col", split_axis=0, concat_axis=2, tiled=True)
    projected_three = jnp.einsum("agce,cf->agfe", spread_three, whole_three, precision=highest)
    block = lax.all_to_all(projected_three, "col", split_axis=2, concat_axis=0, tiled=True)
    columns = block.reshape(first_len, -1)
    basis = factor_init
    local_gram = jnp.dot(columns, columns.T, precision=highest, preferred_element_type=jnp.float32)
    gram = lax.psum(local_gram, ("row", "col"))
    image = jnp.dot(gram, basis, precision=highest, preferred_element_type=jnp.float32)
    square = jnp.dot(image.T, image, precision=highest, preferred_element_type=jnp.float32)
    lower = jnp.linalg.cholesky(square)
    basis = jax.scipy.linalg.solve_triangular(lower, image.T, lower=True).T
    core = jnp.dot(basis.T, columns, precision=highest, preferred_element_type=jnp.float32)
    return (basis, core.reshape(rank_one, block.shape[1], block.shape[2], block.shape[3]))


def solution(mesh):
    in_specs = (P(None, "row", "col"), P("row", None), P("col", None), P(), P())
    out_specs = (P(), P(None, "row", "col", None))
    return jax.shard_map(shards, mesh=mesh, in_specs=in_specs, out_specs=out_specs, check_vma=False)
```

profile of v0, /device:TPU:0, one launch (start us, length us, event | category | flops | bytes accessed | tf_op | source)
XLA Modules:
  0.0 512.5 jit_solution(1816454857235836736)
XLA Ops:
  7.2 5.5 %copy.18 = f32[1024,8,128]{0,2,1:T(8,128)} copy(f32[1024,8,128]{2,1,0:T(8,128)} %param.5) | data formatting | bytes 8388608 | tf_op args[0]
  12.6 4.2 fusion.12
  16.8 12.2 %copy.19 = f32[1024,8,4,16]{3,2,1,0:T(4,128)} copy(f32[1024,8,4,16]{0,3,2,1:T(8,128)S(1)} %fusion.12) | data formatting | bytes 4194304 | tf_op jit(solution)/shard_map/abcd,de->abce/dot_general | solution.py:15
  29.0 15.5 %reshape.31 = f32[4,1,131072]{2,1,0:T(1,128)} reshape(f32[1024,8,4,16]{3,2,1,0:T(4,128)} %copy.19) | data formatting | bytes 4194304
  44.5 4.4 all-to-all-start
  48.9 26.7 %all_gather.6 = f32[32,32]{1,0:T(8,128)S(1)} all-gather(f32[8,32]{1,0:T(8,128)S(1)} %copy-done.5), channel_id=1, replica_groups=mesh['row'=4,'col'=8] {'row'}, dimensions={0}, use_global_device_ids=true | all-gather | bytes 5120 | tf_op jit(solution)/shard_map/all_gather | solution.py:16
  75.5 1.4 copy-done.2
  77.4 7.7 %reduce.6 = f32[4,131072]{1,0:T(4,128)S(1)} reduce(f32[4,1,131072]{2,1,0:T(1,128)} %copy-done.2, f32[]{:T(128)} %broadcast.53), dimensions={1}, to_apply=%all_to_all.50.reduce_sub_computation | reduce | bytes 4194308 | tf_op jit(solution)/shard_map/all_to_all | solution.py:17
  85.1 17.9 %reshape.32 = f32[1024,8,4,16]{3,2,1,0:T(4,128)} reshape(f32[4,131072]{1,0:T(4,128)S(1)} %reduce.6) | data formatting | bytes 4194304
  103.0 12.2 %copy.20 = f32[4,256,8,4,16]{1,2,0,4,3:T(8,128)S(1)} copy(f32[4,256,8,4,16]{4,3,2,1,0:T(4,128)} %bitcast.72) | data formatting | bytes 4194304 | tf_op jit(solution)/shard_map/all_to_all | solution.py:17
  115.3 1.9 fusion.2
  117.2 1.2 copy.21
  118.4 28.1 %all_to_all.69 = f32[256,32,4,16]{0,3,2,1:T(8,128)S(1)} all-to-all(f32[256,32,4,16]{0,3,2,1:T(8,128)S(1)} %copy.21), channel_id=1, replica_groups=mesh['row'=4,'col'=8] {'row'}, dimensions={1} | all-to-all | bytes 4194304 | tf_op jit(solution)/shard_map/all_to_all | solution.py:19
  146.6 12.1 %copy.37 = f32[256,4,8,4,16]{4,3,2,0,1:T(4,128)} copy(f32[256,4,8,4,16]{0,4,3,2,1:T(8,128)S(1)} %bitcast.78) | data formatting | bytes 4194304 | tf_op jit(solution)/shard_map/all_to_all | solution.py:19
  158.6 15.4 %reshape.33 = f32[8,1,65536]{2,1,0:T(1,128)} reshape(f32[1024,8,4,16]{3,2,1,0:T(4,128)} %bitcast.73) | data formatting | bytes 4194304
  174.0 6.8 %all-to-all-start.2 = ((f32[8,1,65536]{2,1,0:T(1,128)}), f32[8,1,65536]{2,1,0:T(1,128)}, u32[]{:S(2)}, u32[]{:S(2)}) async-start(f32[8,1,65536]{2,1,0:T(1,128)} %reshape.33), calls=%async_computation.2 | async-start | bytes 4194304 | tf_op jit(solution)/shard_map/all_to_all | solution.py:21
  180.9 66.5 %all-gather = f32[8,4,32]{2,1,0:T(4,128)S(1)} all-gather(f32[1,4,32]{2,1,0:T(4,128)S(1)} %bitcast.85), channel_id=1, replica_groups=mesh['row'=4,'col'=8] {'col'}, dimensions={0}, use_global_device_ids=true | all-gather | bytes 4608 | tf_op jit(solution)/shard_map/all_gather | solution.py:20
  247.3 7.2 %reduce.7 = f32[8,65536]{1,0:T(8,128)S(1)} reduce(f32[8,1,65536]{2,1,0:T(1,128)} %all-to-all-done.2, f32[]{:T(128)} %broadcast.53), dimensions={1}, to_apply=%all_to_all.58.reduce_sub_computation | reduce | bytes 4194308 | tf_op jit(solution)/shard_map/all_to_all | solution.py:21
  254.6 17.3 %reshape.34 = f32[1024,8,4,16]{3,2,1,0:T(4,128)} reshape(f32[8,65536]{1,0:T(8,128)S(1)} %reduce.7) | data formatting | bytes 4194304
  271.9 9.8 %copy.35 = f32[8,128,8,4,16]{1,0,4,3,2:T(8,128)S(1)} copy(f32[8,128,8,4,16]{4,3,2,1,0:T(4,128)} %bitcast.74) | data formatting | bytes 4194304 | tf_op jit(solution)/shard_map/all_to_all | solution.py:21
  281.7 1.4 copy.25
  283.1 1.9 convolution_bitcast_fusion
  285.0 1.2 copy.27
  286.2 46.2 %all_to_all.70 = f32[128,8,32,16]{0,3,1,2:T(8,128)S(1)} all-to-all(f32[128,8,32,16]{0,3,1,2:T(8,128)S(1)} %copy.27), channel_id=1, replica_groups=mesh['row'=4,'col'=8] {'col'}, dimensions={2} | all-to-all | bytes 4194304 | tf_op jit(solution)/shard_map/all_to_all | solution.py:23
  332.5 1.2 copy.28
  333.7 8.9 %fusion.14 = f32[1024,1024]{1,0:T(8,128)} fusion(f32[64,8,8,128]{3,2,1,0:T(8,128)S(1)} %bitcast.75), kind=kOutput, calls=%fused_computation.20 | convolution fusion | flops 6442450944 | bytes 6291456 | tf_op jit(solution)/shard_map/dot_general | solution.py:26
  342.7 1.9 copy.41
  344.5 138.8 %all-reduce.2.cloned.1.call-done = f32[1024,1024]{1,0:T(8,128)} async-done(((f32[1024,1024]{1,0:T(8,128)}), f32[1024,1024]{1,0:T(8,128)}) %all-reduce.2.cloned.1.call-update) | async-done | bytes 4194320 | tf_op jit(solution)/shard_map/psum | solution.py:27
  483.4 6.3 %fusion.15 = f32[1024,64]{0,1:T(8,128)S(1)} fusion(f32[1024,1024]{1,0:T(8,128)} %all-reduce.2.cloned.1.call-done, f32[1024,64]{0,1:T(8,128)S(1)} %copy-done), kind=kOutput, calls=%fused_computation.21 | convolution fusion | flops 805306368 | bytes 4718592 | tf_op jit(solution)/shard_map/dot_general | solution.py:28
  490.2 5.8 %cholesky.16 = f32[64,64]{1,0:T(8,128)S(1)} custom-call(f32[64,64]{1,0:T(8,128)S(1)} %fusion.10), custom_call_target="Cholesky" | custom-call | tf_op jit(solution)/shard_map/jit(cholesky)/cholesky | solution.py:30
  497.3 4.9 custom-call.7
  502.7 2.5 fusion.5
  (25 shorter events, 2.8 us)
Async XLA Ops:
  7.2 476.2 %copy-start = (f32[1024,64]{0,1:T(8,128)S(1)}, f32[1024,64]{0,1:T(8,128)}, u32[]{:S(2)}) copy-start(f32[1024,64]{0,1:T(8,128)} %param.9) | copy-start | bytes 786436
  7.2 5.5 %copy-start.4 = (f32[32,16]{0,1:T(8,128)S(1)}, f32[32,16]{0,1:T(8,128)}, u32[]{:S(2)}) copy-start(f32[32,16]{0,1:T(8,128)} %param.8) | copy-start | bytes 6148
  44.5 4.4 copy-start.5
  44.5 31.1 %all-to-all-start = ((f32[4,1,131072]{2,1,0:T(1,128)}), f32[4,1,131072]{2,1,0:T(1,128)S(1)}, u32[]{:S(2)}, u32[]{:S(2)}) async-start(f32[4,1,131072]{2,1,0:T(1,128)} %reshape.31), calls=%async_computation | async-start | bytes 4194304 | tf_op jit(solution)/shard_map/all_to_all | solution.py:17
  75.5 1.4 copy-start.2
  174.0 6.8 %copy-start.6 = (f32[4,32]{1,0:T(4,128)S(1)}, f32[4,32]{1,0:T(4,128)}, u32[]{:S(2)}) copy-start(f32[4,32]{1,0:T(4,128)} %param.7) | copy-start | bytes 1540
  174.0 73.3 %all-to-all-start.2 = ((f32[8,1,65536]{2,1,0:T(1,128)}), f32[8,1,65536]{2,1,0:T(1,128)}, u32[]{:S(2)}, u32[]{:S(2)}) async-start(f32[8,1,65536]{2,1,0:T(1,128)} %reshape.33), calls=%async_computation.2 | async-start | bytes 4194304 | tf_op jit(solution)/shard_map/all_to_all | solution.py:21
  180.8 302.5 %all-reduce.2.cloned.1.call-start = ((), (), s32[]{:S(2)}) async-start(), calls=%async_computation.4 | async-start | bytes 8388608 | tf_op jit(solution)/shard_map/psum | solution.py:27
  344.5 158.2 %copy-start.1 = (f32[64,8,8,128]{3,1,2,0:T(8,128)S(1)}, f32[64,8,8,128]{3,1,2,0:T(8,128)}, u32[]{:S(2)}) copy-start(f32[64,8,8,128]{3,1,2,0:T(8,128)} %copy.41) | copy-start | bytes 6291460
  502.7 2.5 copy-start.3
Sparse Core Ops, SparseCore 0:
  342.8 140.5 all-reduce.1
where the time goes:
time: 518 us; the launch traced here: 512 us
  blocking collectives  168 us (32%)
  waiting for transfers between devices  139 us (27%)
  local copies, waits for them, and re-layouts  127 us (25%)
  other arithmetic  27 us (5%)
  matrix products  26.5 us (5%)
  between operations  14.6 us (3%)
  starting transfers between devices  11.2 us (2%)
    psum x1, waiting for transfers between devices, shards(): gram = lax.psum(local_gram, ('row', 'col'))  139 us
    unnamed x20, local copies, waits for them, and re-layouts  74.8 us
    all_gather x1, blocking collectives, shards(): whole_three = lax.all_gather(factor_three, 'col', axis=0, tiled=True)  66.5 us
    all_to_all x1, blocking collectives, shards(): lax.all_to_all(projected_three, 'col', split_axis=2, concat_axis=0, tiled...  46.2 us
    all_to_all x1, blocking collectives, shards(): lax.all_to_all(projected_two, 'row', split_axis=1, concat_axis=0, tiled=T...  28.1 us
    all_gather x1, blocking collectives, shards(): whole_two = lax.all_gather(factor_two, 'row', axis=0, tiled=True)  26.7 us
    all_to_all x2, local copies, waits for them, and re-layouts, shards(): lax.all_to_all(fourth, 'row', split_axis=0, concat_axis=1, tiled=True)  12.7 us
    dot_general x1, local copies, waits for them, and re-layouts, shards(): fourth = jnp.einsum('abcd,de->abce', data, factor_four, precision=highest)  12.2 us
  transfers between devices with their start and end apart: 3, of which 1 were waited for; matrix products, arithmetic and copies ran while one was open for 0% of the time, Pallas kernels for 0%

commit v1 on v0

--- a/solution.py
+++ b/solution.py
@@ -16,7 +16,15 @@
     whole_two = lax.all_gather(factor_two, "row", axis=0, tiled=True)
     spread_two = lax.all_to_all(fourth, "row", split_axis=0, concat_axis=1, tiled=True)
     projected_two = jnp.einsum("abce,bg->agce", spread_two, whole_two, precision=highest)
-    partial_two = lax.all_to_all(projected_two, "row", split_axis=1, concat_axis=0, tiled=True)
+    ways, here = (lax.axis_size("row"), lax.axis_index("row"))
+    width = projected_two.shape[1] // ways
+    turned = jnp.roll(projected_two, -here * width, axis=1)
+    got = [lax.slice_in_dim(turned, 0, width, axis=1)]
+    for far in range(1, ways):
+        sent = lax.slice_in_dim(turned, far * width, (far + 1) * width, axis=1)
+        got.append(lax.ppermute(sent, "row", [(d, (d + far) % ways) for d in range(ways)]))
+    line = jnp.concatenate(got[::-1], axis=0)
+    partial_two = jnp.roll(line, (here + 1) * got[0].shape[0], axis=0)
     whole_three = lax.all_gather(factor_three, "col", axis=0, tiled=True)
     spread_three = lax.all_to_all(partial_two, "col", split_axis=0, concat_axis=2, tiled=True)
     projected_three = jnp.einsum("agce,cf->agfe", spread_three, whole_three, precision=highest)

time: 518 us -> 511 us (0.986)
  blocking collectives: 168 us -> 138 us
  waiting for transfers between devices: 139 us -> 164 us
    all_to_all x1 -> x0, blocking collectives: 28.1 us -> none  [shards(): lax.all_to_all(projected_two, 'row', split_axis=1, concat_axis=0, tiled=T...]
    ppermute x0 -> x3, waiting for transfers between devices: none -> 23.8 us  [shards(): lax.ppermute(sent, 'row', [(d, (d + far) % ways) for d in range(ways)])]
    dynamic_slice x0 -> x2, local copies, waits for them, and re-layouts: none -> 13.8 us  [shards(): partial_two = jnp.roll(line, (here + 1) * got[0].shape[0], axis=0)]
    all_to_all x1 -> x0, local copies, waits for them, and re-layouts: 12.1 us -> none  [shards(): lax.all_to_all(projected_two, 'row', split_axis=1, concat_axis=0, tiled=T...]
    unnamed x20 -> x27, local copies, waits for them, and re-layouts: 74.8 us -> 67.1 us
    all_to_all x2 -> x1, local copies, waits for them, and re-layouts: 11.2 us -> 12.3 us  [shards(): lax.all_to_all(partial_two, 'col', split_axis=0, concat_axis=2, tiled=True)]
  transfers between devices with their start and end apart: 3 -> 6, of which waited for: 1 -> 3; matrix products, arithmetic and copies ran while one was open for 0% -> 0% of each run, Pallas kernels for 0% -> 0%
where the time goes in v1:
time: 511 us; the launch traced here: 505 us
  waiting for transfers between devices  164 us (32%)
  blocking collectives  138 us (27%)
  local copies, waits for them, and re-layouts  122 us (24%)
  other arithmetic  27.5 us (5%)
  matrix products  26.5 us (5%)
  between operations  14.5 us (3%)
  starting transfers between devices  13.2 us (3%)
    psum x1, waiting for transfers between devices, shards(): gram = lax.psum(local_gram, ('row', 'col'))  140 us
    unnamed x27, local copies, waits for them, and re-layouts  67.1 us
    all_gather x1, blocking collectives, shards(): whole_three = lax.all_gather(factor_three, 'col', axis=0, tiled=True)  64.6 us
    all_to_all x1, blocking collectives, shards(): lax.all_to_all(projected_three, 'col', split_axis=2, concat_axis=0, tiled...  46.2 us
    all_gather x1, blocking collectives, shards(): whole_two = lax.all_gather(factor_two, 'row', axis=0, tiled=True)  26.7 us
    ppermute x3, waiting for transfers between devices, shards(): lax.ppermute(sent, 'row', [(d, (d + far) % ways) for d in range(ways)])  23.8 us
    dynamic_slice x2, local copies, waits for them, and re-layouts, shards(): partial_two = jnp.roll(line, (here + 1) * got[0].shape[0], axis=0)  13.8 us
    all_to_all x2, local copies, waits for them, and re-layouts, shards(): lax.all_to_all(fourth, 'row', split_axis=0, concat_axis=1, tiled=True)  12.7 us
  transfers between devices with their start and end apart: 6, of which 3 were waited for; matrix products, arithmetic and copies ran while one was open for 0% of the time, Pallas kernels for 0%

profile of v1, /device:TPU:0, one launch (start us, length us, event | category | flops | bytes accessed | tf_op | source)
XLA Modules:
  0.0 505.1 jit_solution(15463481393535666238)
XLA Ops:
  7.2 5.5 %copy.27 = f32[1024,8,128]{0,2,1:T(8,128)} copy(f32[1024,8,128]{2,1,0:T(8,128)} %param.5) | data formatting | bytes 8388608 | tf_op args[0]
  12.7 4.2 fusion.13
  16.8 12.2 %copy.28 = f32[1024,8,4,16]{3,2,1,0:T(4,128)} copy(f32[1024,8,4,16]{0,3,2,1:T(8,128)S(1)} %fusion.13) | data formatting | bytes 4194304 | tf_op jit(solution)/shard_map/abcd,de->abce/dot_general | solution.py:15
  29.0 15.5 %reshape.31 = f32[4,1,131072]{2,1,0:T(1,128)} reshape(f32[1024,8,4,16]{3,2,1,0:T(4,128)} %copy.28) | data formatting | bytes 4194304
  44.5 4.4 all-to-all-start
  48.9 26.7 %all_gather.6 = f32[32,32]{1,0:T(8,128)S(1)} all-gather(f32[8,32]{1,0:T(8,128)S(1)} %copy-done.5), channel_id=1, replica_groups=mesh['row'=4,'col'=8] {'row'}, dimensions={0}, use_global_device_ids=true | all-gather | bytes 5120 | tf_op jit(solution)/shard_map/all_gather | solution.py:16
  75.6 1.3 copy-done.2
  77.4 7.7 %reduce.6 = f32[4,131072]{1,0:T(4,128)S(1)} reduce(f32[4,1,131072]{2,1,0:T(1,128)} %copy-done.2, f32[]{:T(128)} %broadcast.55), dimensions={1}, to_apply=%all_to_all.37.reduce_sub_computation | reduce | bytes 4194308 | tf_op jit(solution)/shard_map/all_to_all | solution.py:17
  85.1 17.7 %reshape.32 = f32[1024,8,4,16]{3,2,1,0:T(4,128)} reshape(f32[4,131072]{1,0:T(4,128)S(1)} %reduce.6) | data formatting | bytes 4194304
  102.8 12.2 %copy.29 = f32[4,256,8,4,16]{1,2,0,4,3:T(8,128)S(1)} copy(f32[4,256,8,4,16]{4,3,2,1,0:T(4,128)} %bitcast.70) | data formatting | bytes 4194304 | tf_op jit(solution)/shard_map/all_to_all | solution.py:17
  115.1 1.9 fusion.3
  119.1 1.6 collective-permute-start.1
  120.7 11.0 %collective-permute-done = f32[256,8,4,16]{0,1,3,2:T(8,128)S(1)} collective-permute-done((f32[256,8,4,16]{0,1,3,2:T(8,128)}, f32[256,8,4,16]{0,1,3,2:T(8,128)S(1)}, u32[]{:S(2)}, u32[]{:S(2)}) %collective-permute-start) | collective-permute-done | bytes 524320 | tf_op jit(solution)/shard_map/ppermute | solution.py:25
  131.8 12.8 %collective-permute-done.1 = f32[256,8,4,16]{0,1,3,2:T(8,128)S(1)} collective-permute-done((f32[256,8,4,16]{0,1,3,2:T(8,128)}, f32[256,8,4,16]{0,1,3,2:T(8,128)S(1)}, u32[]{:S(2)}, u32[]{:S(2)}) %collective-permute-start.1) | collective-permute-done | bytes 524320 | tf_op jit(solution)/shard_map/ppermute | solution.py:25
  147.2 13.7 %copy.30 = f32[1024,8,4,16]{3,1,2,0:T(8,128)} copy(f32[1024,8,4,16]{0,1,3,2:T(8,128)S(1)} %constant_dynamic-slice_fusion) | data formatting | bytes 4194304 | tf_op jit(solution)/shard_map/jit(_roll_dynamic)/dynamic_slice | solution.py:27
  160.8 11.6 %reshape.33 = f32[8,1,65536]{2,1,0:T(1,128)} reshape(f32[1024,4,8,16]{3,2,1,0:T(8,128)} %bitcast.71) | data formatting | bytes 4194304
  172.4 6.8 %all-to-all-start.1 = ((f32[8,1,65536]{2,1,0:T(1,128)}), f32[8,1,65536]{2,1,0:T(1,128)}, u32[]{:S(2)}, u32[]{:S(2)}) async-start(f32[8,1,65536]{2,1,0:T(1,128)} %reshape.33), calls=%async_computation.1 | async-start | bytes 4194304 | tf_op jit(solution)/shard_map/all_to_all | solution.py:29
  179.3 64.6 %all-gather = f32[8,4,32]{2,1,0:T(4,128)S(1)} all-gather(f32[1,4,32]{2,1,0:T(4,128)S(1)} %bitcast.81), channel_id=1, replica_groups=mesh['row'=4,'col'=8] {'col'}, dimensions={0}, use_global_device_ids=true | all-gather | bytes 4608 | tf_op jit(solution)/shard_map/all_gather | solution.py:28
  243.9 7.2 %reduce.7 = f32[8,65536]{1,0:T(8,128)S(1)} reduce(f32[8,1,65536]{2,1,0:T(1,128)} %all-to-all-done.1, f32[]{:T(128)} %broadcast.55), dimensions={1}, to_apply=%all_to_all.41.reduce_sub_computation | reduce | bytes 4194308 | tf_op jit(solution)/shard_map/all_to_all | solution.py:29
  251.1 11.2 %reshape.34 = f32[1024,4,8,16]{3,2,1,0:T(8,128)} reshape(f32[8,65536]{1,0:T(8,128)S(1)} %reduce.7) | data formatting | bytes 4194304
  262.3 12.3 %copy.31 = f32[8,128,8,4,16]{1,3,0,4,2:T(4,128)S(1)} copy(f32[8,128,8,4,16]{4,2,3,1,0:T(8,128)} %bitcast.72) | data formatting | bytes 4194304 | tf_op jit(solution)/shard_map/all_to_all | solution.py:29
  274.6 1.9 convolution_bitcast_fusion
  276.6 1.2 copy.33
  277.8 46.2 %all_to_all.51 = f32[128,8,32,16]{0,3,1,2:T(8,128)S(1)} all-to-all(f32[128,8,32,16]{0,3,1,2:T(8,128)S(1)} %copy.33), channel_id=1, replica_groups=mesh['row'=4,'col'=8] {'col'}, dimensions={2} | all-to-all | bytes 4194304 | tf_op jit(solution)/shard_map/all_to_all | solution.py:31
  324.0 1.2 copy.34
  325.3 8.9 %fusion.15 = f32[1024,1024]{1,0:T(8,128)} fusion(f32[64,8,8,128]{3,2,1,0:T(8,128)S(1)} %bitcast.73), kind=kOutput, calls=%fused_computation.32 | convolution fusion | flops 6442450944 | bytes 6291456 | tf_op jit(solution)/shard_map/dot_general | solution.py:34
  334.2 1.8 copy.44
  336.0 140.1 %all-reduce.2.cloned.1.call-done = f32[1024,1024]{1,0:T(8,128)} async-done(((f32[1024,1024]{1,0:T(8,128)}), f32[1024,1024]{1,0:T(8,128)}) %all-reduce.2.cloned.1.call-update) | async-done | bytes 4194320 | tf_op jit(solution)/shard_map/psum | solution.py:35
  476.2 6.3 %fusion.17 = f32[1024,64]{0,1:T(8,128)S(1)} fusion(f32[1024,1024]{1,0:T(8,128)} %all-reduce.2.cloned.1.call-done, f32[1024,64]{0,1:T(8,128)S(1)} %copy-done), kind=kOutput, calls=%fused_computation.34 | convolution fusion | flops 805306368 | bytes 4718592 | tf_op jit(solution)/shard_map/dot_general | solution.py:36
  483.0 5.8 %cholesky.16 = f32[64,64]{1,0:T(8,128)S(1)} custom-call(f32[64,64]{1,0:T(8,128)S(1)} %fusion.11), custom_call_target="Cholesky" | custom-call | tf_op jit(solution)/shard_map/jit(cholesky)/cholesky | solution.py:38
  490.1 4.9 custom-call.7
  495.5 2.5 fusion.6
  (39 shorter events, 7.5 us)
Async XLA Ops:
  7.2 469.0 %copy-start = (f32[1024,64]{0,1:T(8,128)S(1)}, f32[1024,64]{0,1:T(8,128)}, u32[]{:S(2)}) copy-start(f32[1024,64]{0,1:T(8,128)} %param.9) | copy-start | bytes 786436
  7.2 5.5 %copy-start.4 = (f32[32,16]{0,1:T(8,128)S(1)}, f32[32,16]{0,1:T(8,128)}, u32[]{:S(2)}) copy-start(f32[32,16]{0,1:T(8,128)} %param.8) | copy-start | bytes 6148
  44.5 4.4 copy-start.5
  44.5 31.1 %all-to-all-start = ((f32[4,1,131072]{2,1,0:T(1,128)}), f32[4,1,131072]{2,1,0:T(1,128)S(1)}, u32[]{:S(2)}, u32[]{:S(2)}) async-start(f32[4,1,131072]{2,1,0:T(1,128)} %reshape.31), calls=%async_computation | async-start | bytes 4194304 | tf_op jit(solution)/shard_map/all_to_all | solution.py:17
  75.5 1.3 copy-start.2
  118.7 13.0 %collective-permute-start = (f32[256,8,4,16]{0,1,3,2:T(8,128)}, f32[256,8,4,16]{0,1,3,2:T(8,128)S(1)}, u32[]{:S(2)}, u32[]{:S(2)}) collective-permute-start(f32[256,8,4,16]{0,1,3,2:T(8,128)} %get-tuple-element.4), channel_id=1, source_target_pairs={{0,24},{8,0},{16,8},{24,16},{1,25},{9,1},{17,9},{25,17},{2,26},{10... | collective-permute-start | bytes 1572872 | tf_op jit(solution)/shard_map/ppermute | solution.py:25
  119.1 25.5 %collective-permute-start.1 = (f32[256,8,4,16]{0,1,3,2:T(8,128)}, f32[256,8,4,16]{0,1,3,2:T(8,128)S(1)}, u32[]{:S(2)}, u32[]{:S(2)}) collective-permute-start(f32[256,8,4,16]{0,1,3,2:T(8,128)} %get-tuple-element.3), channel_id=1, source_target_pairs={{0,16},{8,24},{16,0},{24,8},{1,17},{9,25},{17,1},{25,9},{2,18},{10... | collective-permute-start | bytes 1572872 | tf_op jit(solution)/shard_map/ppermute | solution.py:25
  120.7 23.9 %collective-permute-start.2 = (f32[256,8,4,16]{0,1,3,2:T(8,128)}, f32[256,8,4,16]{0,1,3,2:T(8,128)}, u32[]{:S(2)}, u32[]{:S(2)}) collective-permute-start(f32[256,8,4,16]{0,1,3,2:T(8,128)} %get-tuple-element.2), channel_id=1, source_target_pairs={{0,8},{8,16},{16,24},{24,0},{1,9},{9,17},{17,25},{25,1},{2,10},{10... | collective-permute-start | bytes 1572872 | tf_op jit(solution)/shard_map/ppermute | solution.py:25
  172.4 6.8 %copy-start.6 = (f32[4,32]{1,0:T(4,128)S(1)}, f32[4,32]{1,0:T(4,128)}, u32[]{:S(2)}) copy-start(f32[4,32]{1,0:T(4,128)} %param.7) | copy-start | bytes 1540
  172.4 71.4 %all-to-all-start.1 = ((f32[8,1,65536]{2,1,0:T(1,128)}), f32[8,1,65536]{2,1,0:T(1,128)}, u32[]{:S(2)}, u32[]{:S(2)}) async-start(f32[8,1,65536]{2,1,0:T(1,128)} %reshape.33), calls=%async_computation.1 | async-start | bytes 4194304 | tf_op jit(solution)/shard_map/all_to_all | solution.py:29
  179.2 296.9 %all-reduce.2.cloned.1.call-start = ((), (), s32[]{:S(2)}) async-start(), calls=%async_computation.3 | async-start | bytes 8388608 | tf_op jit(solution)/shard_map/psum | solution.py:35
  336.0 159.5 %copy-start.1 = (f32[64,8,8,128]{3,1,2,0:T(8,128)S(1)}, f32[64,8,8,128]{3,1,2,0:T(8,128)}, u32[]{:S(2)}) copy-start(f32[64,8,8,128]{3,1,2,0:T(8,128)} %copy.44) | copy-start | bytes 6291460
  495.5 2.5 copy-start.3
Sparse Core Ops, SparseCore 0:
  334.3 141.7 all-reduce.1
